TPU v7x, 32 devices: a 4x4x1 block of a 4x4x8 slice. The times are simulated.
32 devices in a mesh: data: 1 (over z), seq: 32 (over y, x, core).
Axes of the slice: x: 4, y: 4, z: 1, core: 2. Of those that a mesh axis runs over, the one named last changes fastest.
The devices are a block of a 4x4x8 slice.
Arguments:
- act_in: bfloat16 [32, 1024, 1024], P('data', 'seq')
- ln1_scale: float32 [1024], replicated
- ln1_bias: float32 [1024], replicated
- w_in: bfloat16 [1024, 4096], replicated
- b_in: float32 [4096], replicated
- ln2_scale: float32 [2048], replicated
- ln2_bias: float32 [2048], replicated
- w_spatial: bfloat16 [1024, 1024], replicated
- b_spatial: float32 [1024], replicated
- causal_mask: int32 [1024, 1024], replicated
- w_out: bfloat16 [2048, 1024], replicated
- b_out: float32 [1024], replicated
Outputs:
- output: bfloat16 [32, 1024, 1024], P('data', 'seq')
All inputs are finite; a program needn't handle non-finite values.
Results may differ from a plain program's by a relative error of at most 0.0115154.
Values are sent between devices in bfloat16 or wider.
A program may use at most 768 MiB of HBM per device.

v0:
```python
import jax
import jax.numpy as jnp
from jax import lax
from jax.sharding import PartitionSpec as P

LN_EPS = 1e-6


def layer_norm(features, ln_gain, ln_shift):
    mean_val = jnp.mean(features, axis=-1, keepdims=True)
    centered = features - mean_val
    var_val = jnp.mean(centered * centered, axis=-1, keepdims=True)
    return centered * lax.rsqrt(var_val + LN_EPS) * ln_gain + ln_shift


def solution(mesh):
    row_spec = P('data', 'seq', None)
    replicated = P()

    def local_block(act_in, ln1_scale, ln1_bias, w_in, b_in, ln2_scale, ln2_bias, w_spatial, b_spatial, causal_mask, w_out, b_out):
        gate_dim = w_out.shape[0]
        normed = layer_norm(act_in.astype(jnp.float32), ln1_scale, ln1_bias).astype(jnp.bfloat16)
        hidden = jax.nn.gelu(jnp.einsum('bsd,df->bsf', normed, w_in, preferred_element_type=jnp.float32) + b_in, approximate=True).astype(jnp.bfloat16)
        gate_half = hidden[:, :, :gate_dim]
        value_norm = layer_norm(hidden[:, :, gate_dim:].astype(jnp.float32), ln2_scale, ln2_bias).astype(jnp.bfloat16)
        value_cols = lax.all_to_all(value_norm, 'seq', 2, 1, tiled=True)
        w_masked = jnp.where(causal_mask > 0, w_spatial, jnp.zeros_like(w_spatial))
        spatial_cols = (jnp.einsum('ij,bjc->bic', w_masked, value_cols, preferred_element_type=jnp.float32) + b_spatial[None, :, None]).astype(jnp.bfloat16)
        spatial_rows = lax.all_to_all(spatial_cols, 'seq', 1, 2, tiled=True)
        gated_act = (gate_half.astype(jnp.float32) * spatial_rows.astype(jnp.float32)).astype(jnp.bfloat16)
        projected = jnp.einsum('bsc,cd->bsd', gated_act, w_out, preferred_element_type=jnp.float32) + b_out
        return (act_in.astype(jnp.float32) + projected).astype(jnp.bfloat16)

    return jax.shard_map(local_block, mesh=mesh, in_specs=(row_spec,) + (replicated,) * 11, out_specs=row_spec, check_vma=False)
```

profile of v0, /device:TPU:97, one launch (start us, length us, event | category | flops | bytes accessed | tf_op | source)
XLA Modules:
  0.0 363.8 jit_solution(3563663672969839619)
XLA Ops:
  0.0 1.9 convert_reduce_fusion.1
  1.9 2.3 fusion.18
  4.3 16.7 %fusion.7 = bf16[32,32,4096]{2,1,0:T(8,128)(2,1)S(1)} fusion(f32[4096]{0:T(1024)} %param.16, bf16[1024,4096]{1,0:T(8,128)(2,1)} %param.15, bf16[32,32,1024]{2,1,0:T(8,128)(2,1)} %param.12, f32[1024]{0:T(1024)} %param.14, f32[1024]{0:T(1024)} %param.13, f32[32,32]{1,0:T(8,128)S(1)} %add_rsqrt_fusion.1, f32[32,32]{1,0:T(8,128)S(1)} %broadcast_multiply_fusion.1), kind=kOutput, calls=%fused_computation.8 | convolution fusion | flops 8638169088 | bytes 18907136 | tf_op jit(solution)/shard_map/bsd,df->bsf/dot_general | solution.py:23
  21.0 0.0 copy-start.2
  21.0 0.0 copy-start.3
  21.0 0.6 convert_reduce_fusion
  21.7 1.4 fusion.10
  23.1 1.1 copy-done
  24.2 3.0 fusion.13
  27.2 23.0 %copy.19 = bf16[32,32,2048]{1,0,2:T(8,128)(2,1)} copy(bf16[32,32,2048]{2,1,0:T(8,128)(2,1)} %fusion.13) | data formatting | bytes 8388608 | tf_op jit(solution)/shard_map/convert_element_type | solution.py:25
  50.2 27.8 %reshape.40 = bf16[32,2,32768]{2,1,0:T(2,128)(2,1)} reshape(bf16[2048,32,32]{2,1,0:T(8,128)(2,1)} %bitcast.30) | data formatting | bytes 8388608
  78.0 61.9 %all_to_all.27 = bf16[32,2,32768]{2,1,0:T(2,128)(2,1)} all-to-all(bf16[32,2,32768]{2,1,0:T(2,128)(2,1)} %reshape.40), channel_id=1, replica_groups=mesh['data'=1,'seq'=32] {'seq'}, dimensions={0} | all-to-all | bytes 8388608 | tf_op jit(solution)/shard_map/all_to_all | solution.py:26
  139.9 24.5 %reshape.41 = bf16[2048,32,32]{2,1,0:T(8,128)(2,1)} reshape(bf16[32,2,32768]{2,1,0:T(2,128)(2,1)} %all_to_all.27) | data formatting | bytes 8388608
  164.3 18.6 %copy.20 = bf16[32,32,32,64]{3,1,2,0:T(8,128)(2,1)} copy(bf16[32,32,32,64]{1,0,3,2:T(8,128)(2,1)} %bitcast.31) | data formatting | bytes 8388608 | tf_op jit(solution)/shard_map/all_to_all | solution.py:26
  182.9 15.5 %fusion.23 = bf16[32,1024,64]{1,2,0:T(8,128)(2,1)} fusion(f32[1024]{0:T(1024)S(1)} %copy-done.5, bf16[32,1024,64]{2,1,0:T(8,128)(2,1)} %bitcast.35, bf16[1024,1024]{1,0:T(8,128)(2,1)S(1)} %copy-done.4, s32[1024,1024]{1,0:T(8,128)} %param.21), kind=kOutput, calls=%fused_computation.32 | convolution fusion | flops 4301258752 | bytes 14684160 | tf_op jit(solution)/shard_map/ij,bjc->bic/dot_general | solution.py:28
  198.4 12.9 %copy.22 = bf16[32,1024,64]{2,0,1:T(8,128)(2,1)} copy(bf16[32,1024,64]{1,2,0:T(8,128)(2,1)} %fusion.23) | data formatting | bytes 8388608 | tf_op jit(solution)/shard_map/convert_element_type | solution.py:28
  211.3 13.9 %reshape.42 = bf16[32,2,32768]{2,1,0:T(2,128)(2,1)} reshape(bf16[1024,32,64]{2,1,0:T(8,128)(2,1)} %bitcast.33) | data formatting | bytes 8388608
  225.2 58.5 %all_to_all.28 = bf16[32,2,32768]{2,1,0:T(2,128)(2,1)} all-to-all(bf16[32,2,32768]{2,1,0:T(2,128)(2,1)} %reshape.42), channel_id=1, replica_groups=mesh['data'=1,'seq'=32] {'seq'}, dimensions={0} | all-to-all | bytes 8388608 | tf_op jit(solution)/shard_map/all_to_all | solution.py:29
  283.7 13.6 %reshape.43 = bf16[1024,32,64]{2,1,0:T(8,128)(2,1)} reshape(bf16[32,2,32768]{2,1,0:T(2,128)(2,1)} %all_to_all.28) | data formatting | bytes 8388608
  297.4 9.8 %copy.23 = bf16[32,1024,64]{2,1,0:T(8,128)(2,1)} copy(bf16[32,1024,64]{2,0,1:T(8,128)(2,1)} %bitcast.34) | data formatting | bytes 8388608 | tf_op jit(solution)/shard_map/all_to_all | solution.py:29
  307.2 11.4 %convert_bitcast_fusion = f32[32,32,32,64]{3,1,2,0:T(8,128)} fusion(bf16[32,32,32,64]{3,2,1,0:T(8,128)(2,1)} %bitcast.32), kind=kLoop, calls=%fused_computation.9 | loop fusion | flops 2097152 | bytes 12582912 | tf_op jit(solution)/shard_map/convert_element_type | solution.py:30
  318.6 18.6 %copy.24 = f32[32,32,32,64]{3,2,1,0:T(8,128)} copy(f32[32,32,32,64]{3,1,2,0:T(8,128)} %convert_bitcast_fusion) | data formatting | bytes 16777216 | tf_op jit(solution)/shard_map/convert_element_type | solution.py:30
  337.2 15.0 %reshape.35 = f32[32,32,2048]{2,1,0:T(8,128)} reshape(f32[32,32,32,64]{3,2,1,0:T(8,128)} %copy.24) | data formatting | bytes 16777216 | tf_op jit(solution)/shard_map/convert_element_type | solution.py:30
  352.1 11.7 %fusion.22 = bf16[32,32,1024]{2,1,0:T(8,128)(2,1)} fusion(bf16[32,32,1024]{2,1,0:T(8,128)(2,1)S(1)} %copy-done.1, f32[1024]{0:T(1024)S(1)} %copy-done.6, bf16[2048,1024]{1,0:T(8,128)(2,1)} %param.22, f32[32,32,2048]{2,1,0:T(8,128)} %reshape.35, bf16[32,32,4096]{2,1,0:T(8,128)(2,1)} %copy-done), kind=kOutput, calls=%fused_computation.31 | convolution fusion | flops 4305453056 | bytes 20975616 | tf_op jit(solution)/shard_map/bsc,cd->bsd/dot_general | solution.py:31
  (15 shorter events, 0.1 us)
Async XLA Ops:
  21.0 3.2 copy-start
  21.0 3.2 copy-start.2
  21.0 3.2 copy-start.3
  164.3 18.6 %copy-start.4 = (bf16[1024,1024]{1,0:T(8,128)(2,1)S(1)}, bf16[1024,1024]{1,0:T(8,128)(2,1)}, u32[]{:S(2)}) copy-start(bf16[1024,1024]{1,0:T(8,128)(2,1)} %param.19) | copy-start | bytes 6291460
  164.3 18.6 %copy-start.5 = (f32[1024]{0:T(1024)S(1)}, f32[1024]{0:T(1024)}, u32[]{:S(2)}) copy-start(f32[1024]{0:T(1024)} %param.20) | copy-start | bytes 12292
  337.2 15.0 %copy-start.1 = (bf16[32,32,1024]{2,1,0:T(8,128)(2,1)S(1)}, bf16[32,32,1024]{2,1,0:T(8,128)(2,1)}, u32[]{:S(2)}) copy-start(bf16[32,32,1024]{2,1,0:T(8,128)(2,1)} %param.12) | copy-start | bytes 6291460
  337.2 15.0 %copy-start.6 = (f32[1024]{0:T(1024)S(1)}, f32[1024]{0:T(1024)}, u32[]{:S(2)}) copy-start(f32[1024]{0:T(1024)} %param.23) | copy-start | bytes 12292
where the time goes:
time: 369 us; the launch traced here: 364 us
  local copies, waits for them, and re-layouts  179 us (49%)
  blocking collectives  120 us (33%)
  matrix products  43.9 us (12%)
  other arithmetic  20.6 us (6%)
    unnamed x18, local copies, waits for them, and re-layouts  80.9 us
    all_to_all x1, blocking collectives, local_block(): value_cols = lax.all_to_all(value_norm, 'seq', 2, 1, tiled=True)  61.9 us
    all_to_all x1, blocking collectives, local_block(): spatial_rows = lax.all_to_all(spatial_cols, 'seq', 1, 2, tiled=True)  58.5 us
    convert_element_type x2, local copies, waits for them, and re-layouts, local_block(): spatial_rows.astype(jnp.float32)  33.5 us
    convert_element_type x1, local copies, waits for them, and re-layouts, local_block(): layer_norm(hidden[:, :, gate_dim:].astype(jnp.float32), ln2_scale, ln2_bias)  23 us
    all_to_all x1, local copies, waits for them, and re-layouts, local_block(): value_cols = lax.all_to_all(value_norm, 'seq', 2, 1, tiled=True)  18.6 us
    dot_general x1, matrix products, local_block(): jnp.einsum('bsd,df->bsf', normed, w_in, preferred_element_type=jnp.float32)  16.7 us
    dot_general x1, matrix products, local_block(): jnp.einsum('ij,bjc->bic', w_masked, value_cols, preferred_element_type=jn...  15.5 us

commit v1 on v0

--- a/solution.py
+++ b/solution.py
@@ -23,10 +23,10 @@
         hidden = jax.nn.gelu(jnp.einsum('bsd,df->bsf', normed, w_in, preferred_element_type=jnp.float32) + b_in, approximate=True).astype(jnp.bfloat16)
         gate_half = hidden[:, :, :gate_dim]
         value_norm = layer_norm(hidden[:, :, gate_dim:].astype(jnp.float32), ln2_scale, ln2_bias).astype(jnp.bfloat16)
-        value_cols = lax.all_to_all(value_norm, 'seq', 2, 1, tiled=True)
+        value_seq = lax.all_to_all(value_norm, 'seq', 0, 1, tiled=True)
         w_masked = jnp.where(causal_mask > 0, w_spatial, jnp.zeros_like(w_spatial))
-        spatial_cols = (jnp.einsum('ij,bjc->bic', w_masked, value_cols, preferred_element_type=jnp.float32) + b_spatial[None, :, None]).astype(jnp.bfloat16)
-        spatial_rows = lax.all_to_all(spatial_cols, 'seq', 1, 2, tiled=True)
+        spatial_seq = (jnp.einsum('ij,bjc->bic', w_masked, value_seq, preferred_element_type=jnp.float32) + b_spatial[None, :, None]).astype(jnp.bfloat16)
+        spatial_rows = lax.all_to_all(spatial_seq, 'seq', 1, 0, tiled=True)
         gated_act = (gate_half.astype(jnp.float32) * spatial_rows.astype(jnp.float32)).astype(jnp.bfloat16)
         projected = jnp.einsum('bsc,cd->bsd', gated_act, w_out, preferred_element_type=jnp.float32) + b_out
         return (act_in.astype(jnp.float32) + projected).astype(jnp.bfloat16)

time: 369 us -> 246 us (0.67)
  local copies, waits for them, and re-layouts: 179 us -> 57.7 us
  matrix products: 43.9 us -> 29.1 us
  other arithmetic: 20.6 us -> 34.8 us
    convert_element_type x4 -> x1, local copies, waits for them, and re-layouts: 69.5 us -> 20.6 us  [local_block(): (jnp.einsum('ij,bjc->bic', w_masked, value_seq, preferred_element_type=jn...]
    unnamed x18 -> x28, local copies, waits for them, and re-layouts: 80.9 us -> 37.1 us
    all_to_all x2 -> x0, local copies, waits for them, and re-layouts: 28.4 us -> none  [the longest x1 18.6 us: local_block(): value_cols = lax.all_to_all(value_norm, 'seq', 2, 1, tiled=True)]
    unnamed x0 -> x1, other arithmetic: none -> 26.7 us
    convert_element_type x1 -> x0, other arithmetic: 11.4 us -> none  [local_block(): spatial_rows.astype(jnp.float32)]
    dot_general x1, matrix products: 15.5 us -> 6.44 us  [local_block(): jnp.einsum('ij,bjc->bic', w_masked, value_seq, preferred_element_type=jnp...]
where the time goes in v1:
time: 246 us; the launch traced here: 242 us
  blocking collectives  120 us (49%)
  local copies, waits for them, and re-layouts  57.7 us (23%)
  other arithmetic  34.8 us (14%)
  matrix products  29.1 us (12%)
    all_to_all x1, blocking collectives, local_block(): value_seq = lax.all_to_all(value_norm, 'seq', 0, 1, tiled=True)  61.9 us
    all_to_all x1, blocking collectives, local_block(): spatial_rows = lax.all_to_all(spatial_seq, 'seq', 1, 0, tiled=True)  58.5 us
    unnamed x28, local copies, waits for them, and re-layouts  37.1 us
    unnamed x1, other arithmetic  26.7 us
    convert_element_type x1, local copies, waits for them, and re-layouts, local_block(): (jnp.einsum('ij,bjc->bic', w_masked, value_seq, preferred_element_type=jn...  20.6 us
    dot_general x1, matrix products, local_block(): jnp.einsum('bsd,df->bsf', normed, w_in, preferred_element_type=jnp.float32)  14.6 us
    dot_general x1, matrix products, local_block(): jnp.einsum('bsc,cd->bsd', gated_act, w_out, preferred_element_type=jnp.fl...  8.08 us
    dot_general x1, matrix products, local_block(): jnp.einsum('ij,bjc->bic', w_masked, value_seq, preferred_element_type=jnp...  6.44 us

profile of v1, /device:TPU:97, one launch (start us, length us, event | category | flops | bytes accessed | tf_op | source)
XLA Modules:
  0.0 242.2 jit_solution(12454528955846861034)
XLA Ops:
  0.0 2.1 convert_reduce_fusion.1
  2.1 2.3 fusion.19
  4.5 14.6 %fusion.7 = bf16[32,32,4096]{2,1,0:T(8,128)(2,1)S(1)} fusion(f32[4096]{0:T(1024)S(1)} %copy-done.7, bf16[1024,4096]{1,0:T(8,128)(2,1)} %param.15, bf16[32,32,1024]{2,1,0:T(8,128)(2,1)S(1)} %copy-done.1, f32[1024]{0:T(1024)S(1)} %copy-done.8, f32[1024]{0:T(1024)S(1)} %copy-done.9, f32[32,32]{1,0:T(8,128)S(1)} %add_rsqrt_fusion.1, ...), kind=kOutput, calls=%fused_computation.8 | convolution fusion | flops 8638169088 | bytes 18907136 | tf_op jit(solution)/shard_map/bsd,df->bsf/dot_general | solution.py:23
  19.1 0.0 copy-start
  19.1 0.0 copy-start.2
  19.1 0.0 copy-start.3
  19.1 0.6 convert_reduce_fusion
  19.8 1.4 fusion.10
  21.2 1.2 copy-done
  22.3 0.0 copy-done.3
  22.3 1.7 fusion.13
  24.0 0.0 copy-start.4
  24.0 0.0 copy-start.6
  24.1 0.0 copy-start.10
  24.1 61.9 %all_to_all.8 = bf16[32,32,2048]{2,1,0:T(8,128)(2,1)S(1)} all-to-all(bf16[32,32,2048]{2,1,0:T(8,128)(2,1)S(1)} %fusion.13), channel_id=1, replica_groups=mesh['data'=1,'seq'=32] {'seq'}, dimensions={0} | all-to-all | bytes 8388608 | tf_op jit(solution)/shard_map/all_to_all | solution.py:26
  86.0 6.4 %fusion.27 = bf16[1,1024,2048]{1,2,0:T(8,128)(2,1)} fusion(f32[1024]{0:T(1024)S(1)} %copy-done.10, bf16[1024,2048]{1,0:T(8,128)(2,1)S(1)} %bitcast.26, bf16[1024,1024]{1,0:T(8,128)(2,1)S(1)} %copy-done.6, s32[1024,1024]{1,0:T(8,128)S(1)} %copy-done.4), kind=kOutput, calls=%fused_computation.36 | convolution fusion | flops 4301258752 | bytes 14684160 | tf_op jit(solution)/shard_map/ij,bjc->bic/dot_general | solution.py:28
  92.4 20.6 %copy.14 = bf16[1,1024,2048]{2,0,1:T(2,128)(2,1)} copy(bf16[1,1024,2048]{1,2,0:T(8,128)(2,1)} %fusion.27) | data formatting | bytes 8388608 | tf_op jit(solution)/shard_map/convert_element_type | solution.py:28
  113.1 0.5 broadcast.61
  113.6 26.7 %reduce = bf16[1024,2048]{1,0:T(8,128)(2,1)} reduce(bf16[1024,1,2048]{2,1,0:T(2,128)(2,1)} %bitcast.23, bf16[]{:T(256)} %broadcast.61), dimensions={1}, to_apply=%bitcast.20.reduce_sub_computation | reduce | bytes 8388610
  140.2 7.9 %reshape.50 = bf16[32,2,32768]{2,1,0:T(2,128)(2,1)} reshape(bf16[1024,2048]{1,0:T(8,128)(2,1)} %reduce) | data formatting | bytes 8388608
  148.1 58.5 %all_to_all.9 = bf16[32,2,32768]{2,1,0:T(2,128)(2,1)} all-to-all(bf16[32,2,32768]{2,1,0:T(2,128)(2,1)} %reshape.50), channel_id=1, replica_groups=mesh['data'=1,'seq'=32] {'seq'}, dimensions={0} | all-to-all | bytes 8388608 | tf_op jit(solution)/shard_map/all_to_all | solution.py:29
  206.6 19.8 %reshape.51 = bf16[1024,1,2048]{2,1,0:T(2,128)(2,1)} reshape(bf16[32,2,32768]{2,1,0:T(2,128)(2,1)} %all_to_all.9) | data formatting | bytes 8388608
  226.4 7.7 %copy.15 = f32[1,1024,2048]{2,1,0:T(8,128)S(1)} copy(bf16[1,1024,2048]{2,0,1:T(2,128)(2,1)} %bitcast.24) | data formatting | bytes 12582912
  234.1 8.1 %fusion.23 = bf16[32,32,1024]{2,1,0:T(8,128)(2,1)} fusion(bf16[32,32,1024]{2,1,0:T(8,128)(2,1)S(1)} %copy-done.1, f32[1024]{0:T(1024)S(1)} %copy-done.11, bf16[2048,1024]{1,0:T(8,128)(2,1)S(1)} %copy-done.5, f32[32,32,2048]{2,1,0:T(8,128)S(1)} %bitcast.25, bf16[32,32,4096]{2,1,0:T(8,128)(2,1)} %copy-done), kind=kOutput, calls=%fused_computation.31 | convolution fusion | flops 4305453056 | bytes 20975616 | tf_op jit(solution)/shard_map/bsc,cd->bsd/dot_general | solution.py:31
  (20 shorter events, 0.1 us)
Async XLA Ops:
  0.0 4.4 %copy-start.1 = (bf16[32,32,1024]{2,1,0:T(8,128)(2,1)S(1)}, bf16[32,32,1024]{2,1,0:T(8,128)(2,1)}, u32[]{:S(2)}) copy-start(bf16[32,32,1024]{2,1,0:T(8,128)(2,1)} %param.12) | copy-start | bytes 6291460
  0.0 4.4 %copy-start.7 = (f32[4096]{0:T(1024)S(1)}, f32[4096]{0:T(1024)}, u32[]{:S(2)}) copy-start(f32[4096]{0:T(1024)} %param.16) | copy-start | bytes 49156
  0.0 4.4 %copy-start.8 = (f32[1024]{0:T(1024)S(1)}, f32[1024]{0:T(1024)}, u32[]{:S(2)}) copy-start(f32[1024]{0:T(1024)} %param.14) | copy-start | bytes 12292
  0.0 4.4 %copy-start.9 = (f32[1024]{0:T(1024)S(1)}, f32[1024]{0:T(1024)}, u32[]{:S(2)}) copy-start(f32[1024]{0:T(1024)} %param.13) | copy-start | bytes 12292
  19.1 3.2 %copy-start = (bf16[32,32,4096]{2,1,0:T(8,128)(2,1)}, bf16[32,32,4096]{2,1,0:T(8,128)(2,1)S(1)}, u32[]{:S(2)}) copy-start(bf16[32,32,4096]{2,1,0:T(8,128)(2,1)S(1)} %fusion.7) | copy-start | bytes 25165828
  19.1 3.2 %copy-start.2 = (f32[2048]{0:T(1024)S(1)}, f32[2048]{0:T(1024)}, u32[]{:S(2)}) copy-start(f32[2048]{0:T(1024)} %param.18) | copy-start | bytes 24580
  19.1 3.2 %copy-start.3 = (f32[2048]{0:T(1024)S(1)}, f32[2048]{0:T(1024)}, u32[]{:S(2)}) copy-start(f32[2048]{0:T(1024)} %param.17) | copy-start | bytes 24580
  24.0 62.0 %copy-start.4 = (s32[1024,1024]{1,0:T(8,128)S(1)}, s32[1024,1024]{1,0:T(8,128)}, u32[]{:S(2)}) copy-start(s32[1024,1024]{1,0:T(8,128)} %param.21) | copy-start | bytes 12582916
  24.0 62.0 %copy-start.6 = (bf16[1024,1024]{1,0:T(8,128)(2,1)S(1)}, bf16[1024,1024]{1,0:T(8,128)(2,1)}, u32[]{:S(2)}) copy-start(bf16[1024,1024]{1,0:T(8,128)(2,1)} %param.19) | copy-start | bytes 6291460
  24.1 61.9 %copy-start.10 = (f32[1024]{0:T(1024)S(1)}, f32[1024]{0:T(1024)}, u32[]{:S(2)}) copy-start(f32[1024]{0:T(1024)} %param.20) | copy-start | bytes 12292
  226.4 7.7 %copy-start.5 = (bf16[2048,1024]{1,0:T(8,128)(2,1)S(1)}, bf16[2048,1024]{1,0:T(8,128)(2,1)}, u32[]{:S(2)}) copy-start(bf16[2048,1024]{1,0:T(8,128)(2,1)} %param.22) | copy-start | bytes 12582916
  226.4 7.7 %copy-start.11 = (f32[1024]{0:T(1024)S(1)}, f32[1024]{0:T(1024)}, u32[]{:S(2)}) copy-start(f32[1024]{0:T(1024)} %param.23) | copy-start | bytes 12292

commit v2 on v1

v2 whole, which is shorter than its diff:
```python
import functools
import math

import jax
import jax.numpy as jnp
from jax import lax
from jax.experimental import pallas as pl
from jax.experimental.pallas import tpu as pltpu
from jax.sharding import PartitionSpec as P

LN_EPS = 1e-6
MESH = pl.DeviceIdType.MESH
F32 = jnp.float32
BF16 = jnp.bfloat16
CORES = 2
NB = 256
GELU_A = math.sqrt(2.0 / math.pi)


def gelu(a):
    return (0.5 * a) * (1.0 + jnp.tanh(a * (GELU_A + (GELU_A * 0.044715) * (a * a))))


def dot(a, b):
    return jnp.dot(a, b, preferred_element_type=F32)


def kernel(n, side, x_hbm, ln1g, ln1b, wi_hbm, b_in, ln2g, ln2b, ws_hbm, bsp, mk_hbm, wo_hbm, b_out, out_hbm,
           xb, u, wv, wg, wo, wm, mk, vbuf, vn, vall, sb, sr, g, st, acc, bcol, q, ob,
           xsem, vsem, msem, gsem, osem, outsem, st_send, st_recv, dir_send, fw_send, fin):
    me = lax.axis_index("seq")
    c = me % CORES
    x = (me // CORES) % side
    y = me // (CORES * side)
    pos = xb.shape[0] // n
    crows = pos * CORES * side
    dim = xb.shape[1]
    gate = wo.shape[0]
    half = gate // 2
    nrel = side - 1

    def dev(yy, xx, cc):
        return (yy * side + xx) * CORES + cc

    def yof(j):
        return (y + j + 1) % side

    def rows_of(j):
        return pl.ds(pl.multiple_of(yof(j) * crows, crows), crows)

    def msg(d, k=1):
        return pl.ds(pl.multiple_of(d * pos, pos), k * pos)

    def xcopy(j):
        return pltpu.make_async_copy(x_hbm.at[rows_of(j)], xb.at[rows_of(j)], xsem.at[j])
    nv = 4
    vw = gate // nv

    def vcopy(i):
        return pltpu.make_async_copy(wi_hbm.at[:, pl.ds(gate + i * vw, vw)], wv.at[:, pl.ds(i * vw, vw)], vsem.at[i])
    xcopy(0).start()
    for i in range(nv):
        vcopy(i).start()
    for j in range(1, side):
        xcopy(j).start()
    ws_copy = pltpu.make_async_copy(ws_hbm, wm, msem.at[0])
    mk_copy = pltpu.make_async_copy(mk_hbm, mk, msem.at[1])
    wg_copy = pltpu.make_async_copy(wi_hbm.at[:, pl.ds(0, gate)], wg, gsem)
    wo_copy = pltpu.make_async_copy(wo_hbm, wo, osem)

    barrier = pltpu.get_barrier_semaphore()
    peers = [dev(y, (x + dx) % side, cc) for dx in range(1, side) for cc in range(CORES)]
    peers += [dev((y + dy) % side, x, cc) for dy in range(1, side) for cc in range(CORES)]
    peers += [dev(y, x, 1 - c)]
    for p in peers:
        pl.semaphore_signal(barrier, inc=1, device_id={"seq": p}, device_id_type=MESH)

    def remote(src, dst, ssem, rsem, target):
        return pltpu.make_async_remote_copy(src_ref=src, dst_ref=dst, send_sem=ssem, recv_sem=rsem,
                                            device_id={"seq": target}, device_id_type=MESH)

    srcs, dsts = (vn, sb), (vall, sr)
    other = dev(y, x, 1 - c)

    def send_stage(a, h, j, i, start=True):
        xx = (x + i + 1) % side
        k = nrel * j + i
        cp = remote(srcs[a].at[h, msg(dev(yof(j), xx, 0), CORES)], st.at[a, h, k], st_send.at[a, h, k], st_recv.at[a, h, k],
                    dev(y, xx, c))
        return cp

    def send_direct(a, h, d, k):
        return remote(srcs[a].at[h, msg(d)], dsts[a].at[h, msg(me)], dir_send.at[a, h, k], fin.at[a, h, me], d)

    def directs(j):
        if j < nrel:
            return [(dev(yof(j), x, cc), CORES * j + cc) for cc in range(CORES)]
        base = CORES * nrel
        out = [(dev(y, (x + i + 1) % side, cc), base + CORES * i + cc) for i in range(nrel) for cc in range(CORES)]
        return out + [(other, 2 * base)]

    def send_chunk(a, h, j):
        if j < nrel:
            for i in range(nrel):
                send_stage(a, h, j, i).start()
        for d, k in directs(j):
            send_direct(a, h, d, k).start()

    def forward(a, h, j, i, cc):
        k = nrel * j + i
        origin = dev(y, (x + side - i - 1) % side, c)
        return remote(st.at[a, h, k, pl.ds(cc * pos, pos)], dsts[a].at[h, msg(origin)], fw_send.at[a, h, CORES * k + cc],
                      fin.at[a, h, origin], dev(yof(j), x, cc))

    def relay(a, h, j):
        for i in range(nrel):
            send_stage(a, h, j, i).wait_recv()
            for cc in range(CORES):
                forward(a, h, j, i, cc).start()

    def wait_from(a, h, origin):
        remote(srcs[a].at[h, msg(me)], dsts[a].at[h, msg(origin)], dir_send.at[a, h, 0], fin.at[a, h, origin], other).wait_recv()

    def wait_row(a, h, yy):
        def body(k, carry):
            d = yy * (CORES * side) + k

            @pl.when(d != me)
            def _():
                wait_from(a, h, d)
            return carry
        lax.fori_loop(0, CORES * side, body, 0)

    def own(a, h):
        dsts[a][h, msg(me), :] = srcs[a][h, msg(me), :]

    lnr = 64

    def ln1(j):
        base = yof(j) * crows

        def body(k, carry):
            r = pl.ds(pl.multiple_of(base + k * lnr, lnr), lnr)
            v = xb[r, :].astype(F32)
            cen = v - jnp.sum(v, axis=-1, keepdims=True) * (1.0 / dim)
            var = jnp.sum(cen * cen, axis=-1, keepdims=True) * (1.0 / dim)
            u[r, :] = (cen * lax.rsqrt(var + LN_EPS) * ln1g[...] + ln1b[...]).astype(BF16)
            return carry
        lax.fori_loop(0, crows // lnr, body, 0, unroll=2)

    def value_cols(j, lo, hi):
        rows = rows_of(j)

        def body(b, carry):
            cols = pl.ds(pl.multiple_of(b * NB, NB), NB)
            bcols = pl.ds(pl.multiple_of(gate + b * NB, NB), NB)
            vbuf[:, cols] = gelu(dot(u[rows, :], wv[:, cols]) + b_in[:, bcols]).astype(BF16)
            return carry
        lax.fori_loop(lo, hi, body, 0)

    lnr2 = 32

    def ln2(j):
        base = yof(j) * crows

        def body(k, carry):
            r0 = pl.multiple_of(k * lnr2, lnr2)
            v = vbuf[pl.ds(r0, lnr2), :].astype(F32)
            cen = v - jnp.sum(v, axis=-1, keepdims=True) * (1.0 / gate)
            var = jnp.sum(cen * cen, axis=-1, keepdims=True) * (1.0 / gate)
            o = (cen * lax.rsqrt(var + LN_EPS) * ln2g[...] + ln2b[...]).astype(BF16)
            r = pl.ds(pl.multiple_of(base + r0, lnr2), lnr2)
            vn[0, r, :] = o[:, :half]
            vn[1, r, :] = o[:, half:]
            return carry
        lax.fori_loop(0, crows // lnr2, body, 0, unroll=2)

    def gate_chunk(j):
        rows = rows_of(j)
        for h in range(2):
            def body(b, carry):
                cols = pl.ds(pl.multiple_of(b * NB, NB), NB)
                wcols = pl.ds(pl.multiple_of(h * half + b * NB, NB), NB)
                g[h, rows, cols] = gelu(dot(u[rows, :], wg[:, wcols]) + b_in[:, wcols]).astype(BF16)
                return carry
            lax.fori_loop(0, half // NB, body, 0)

    def mask_weights():
        step = 64

        def body(k, carry):
            r = pl.ds(pl.multiple_of(k * step, step), step)
            wm[r, :] = jnp.where(mk[r, :] > 0, wm[r, :].astype(F32), 0.0).astype(BF16)
            return carry
        lax.fori_loop(0, wm.shape[0] // step, body, 0)
        for k in range(bsp.shape[1] // 128):
            blk = jnp.broadcast_to(bsp[:, k * 128:(k + 1) * 128], (128, 128))
            bcol[k * 128:(k + 1) * 128, :] = blk.T

    def spatial(h, j):
        rows = rows_of(j)

        def body(b, carry):
            cols = pl.ds(pl.multiple_of(b * NB, NB), NB)
            sb[h, rows, cols] = (dot(wm[rows, :], vall[h, :, cols]) + bcol[rows, 0:1]).astype(BF16)
            return carry
        lax.fori_loop(0, half // NB, body, 0)

    def gated(h, rows):
        q[...] = (g[h, rows, :].astype(F32) * sr[h, rows, :].astype(F32)).astype(BF16)

    def arrive(j):
        return (y + side - 1 - j) % side

    def arrive_rows(j):
        return pl.ds(pl.multiple_of(arrive(j) * crows, crows), crows)

    def project0(j):
        rows = arrive_rows(j)
        gated(0, rows)

        def body(b, carry):
            cols = pl.ds(pl.multiple_of(b * NB, NB), NB)
            acc[rows, cols] = dot(q[...], wo[:half, cols]) + (b_out[:, cols] + xb[rows, cols].astype(F32))
            return carry
        lax.fori_loop(0, dim // NB, body, 0)

    def out_copy(j):
        return pltpu.make_async_copy(ob.at[arrive_rows(j)], out_hbm.at[arrive_rows(j)], outsem.at[j])

    def project1(j):
        rows = arrive_rows(j)
        gated(1, rows)

        def body(b, carry):
            cols = pl.ds(pl.multiple_of(b * NB, NB), NB)
            ob[rows, cols] = (acc[rows, cols] + dot(q[...], wo[half:, cols])).astype(BF16)
            return carry
        lax.fori_loop(0, dim // NB, body, 0)
        out_copy(j).start()

    for j in range(side):
        xcopy(j).wait()
        ln1(j)
        if j == 0:
            for i in range(nv):
                vcopy(i).wait()
                value_cols(j, i * vw // NB, (i + 1) * vw // NB)
            ws_copy.start()
            mk_copy.start()
            wg_copy.start()
            wo_copy.start()
        else:
            value_cols(j, 0, gate // NB)
        ln2(j)
        if j == 0:
            pl.semaphore_wait(barrier, len(peers))
        send_chunk(0, 0, j)
        if j >= 2:
            relay(0, 0, j - 2)
    for j in range(side):
        send_chunk(0, 1, j)
    own(0, 0)
    own(0, 1)
    wg_copy.wait()
    gate_chunk(0)
    gate_chunk(1)
    relay(0, 0, 2)
    gate_chunk(2)
    gate_chunk(3)
    ws_copy.wait()
    mk_copy.wait()
    mask_weights()
    wo_copy.wait()
    for j in range(side):
        wait_row(0, 0, arrive(j))
    for j in range(side):
        spatial(0, j)
        send_chunk(1, 0, j)
    own(1, 0)
    for j in range(nrel):
        relay(0, 1, j)
    for j in range(side):
        wait_row(0, 1, arrive(j))
    for j in range(side):
        spatial(1, j)
        send_chunk(1, 1, j)
    own(1, 1)
    for j in range(nrel):
        relay(1, 0, j)
    for j in range(side):
        wait_row(1, 0, arrive(j))
        project0(j)
        if j < nrel:
            relay(1, 1, j)
    for j in range(side):
        wait_row(1, 1, arrive(j))
        project1(j)

    for a in range(2):
        for h in range(2):
            for j in range(nrel):
                for i in range(nrel):
                    send_stage(a, h, j, i).wait_send()
                    for cc in range(CORES):
                        forward(a, h, j, i, cc).wait_send()
            for j in range(side):
                for d, k in directs(j):
                    send_direct(a, h, d, k).wait_send()
    for j in range(side):
        out_copy(j).wait()


def solution(mesh):
    n = mesh.shape['seq']
    side = math.isqrt(n // CORES)
    row_spec = P('data', 'seq', None)
    replicated = P()

    def local_block(act_in, ln1_scale, ln1_bias, w_in, b_in, ln2_scale, ln2_bias, w_spatial, b_spatial, causal_mask, w_out, b_out):
        batch, pos, dim = act_in.shape
        gate = w_out.shape[0]
        half = gate // 2
        rows = batch * pos
        seq_len = w_spatial.shape[0]
        crows = pos * CORES * side
        nrel = side - 1
        if batch != n or side * side * CORES != n:
            raise ValueError('unexpected group')
        vm = pl.BlockSpec(memory_space=pltpu.VMEM)
        anyspec = pl.BlockSpec(memory_space=pl.ANY)
        dma = pltpu.SemaphoreType.DMA
        out = pl.pallas_call(
            functools.partial(kernel, n, side),
            out_shape=jax.ShapeDtypeStruct((rows, dim), BF16),
            in_specs=[anyspec, vm, vm, anyspec, vm, vm, vm, anyspec, vm, anyspec, anyspec, vm],
            out_specs=anyspec,
            scratch_shapes=[
                pltpu.VMEM((rows, dim), BF16), pltpu.VMEM((rows, dim), BF16),
                pltpu.VMEM((dim, gate), BF16), pltpu.VMEM((dim, gate), BF16), pltpu.VMEM((gate, dim), BF16),
                pltpu.VMEM((seq_len, seq_len), BF16), pltpu.VMEM((seq_len, seq_len), jnp.int32),
                pltpu.VMEM((crows, gate), BF16),
                pltpu.VMEM((2, rows, half), BF16), pltpu.VMEM((2, seq_len, half), BF16),
                pltpu.VMEM((2, seq_len, half), BF16), pltpu.VMEM((2, rows, half), BF16),
                pltpu.VMEM((2, rows, half), BF16),
                pltpu.VMEM((2, 2, nrel * nrel, CORES * pos, half), BF16),
                pltpu.VMEM((rows, dim), F32), pltpu.VMEM((seq_len, 128), F32),
                pltpu.VMEM((crows, half), BF16), pltpu.VMEM((rows, dim), BF16),
                dma((side,)), dma((4,)), dma((2,)), dma, dma, dma((side,)),
                dma((2, 2, nrel * nrel)), dma((2, 2, nrel * nrel)), dma((2, 2, 2 * CORES * nrel + 1)),
                dma((2, 2, CORES * nrel * nrel)), dma((2, 2, n)),
            ],
            compiler_params=pltpu.CompilerParams(collective_id=0, has_side_effects=True, vmem_limit_bytes=66900000),
            name='gmlp_block',
        )(act_in.reshape(rows, dim), ln1_scale.reshape(1, -1), ln1_bias.reshape(1, -1), w_in, b_in.reshape(1, -1),
          ln2_scale.reshape(1, -1), ln2_bias.reshape(1, -1), w_spatial, b_spatial.reshape(1, -1), causal_mask, w_out,
          b_out.reshape(1, -1))
        return out.reshape(batch, pos, dim)

    return jax.shard_map(local_block, mesh=mesh, in_specs=(row_spec,) + (replicated,) * 11, out_specs=row_spec, check_vma=False)
```

time: 246 us -> 131 us (0.53); the launches traced: 242 us -> 131 us
  Pallas kernels: 0 us -> 128 us
  blocking collectives: 120 us -> 0 us
  local copies, waits for them, and re-layouts: 57.7 us -> 3.19 us
  other arithmetic: 34.8 us -> 0 us
  matrix products: 29.1 us -> 0 us
    pallas_call x0 -> x1, Pallas kernels: none -> 128 us  [local_block(): pl.pallas_call(functools.partial(kernel, n, side), out_shape=jax.ShapeDty...]
    all_to_all x2 -> x0, blocking collectives: 120 us -> none  [the longest x1 61.9 us: local_block(): value_seq = lax.all_to_all(value_norm, 'seq', 0, 1, tiled=True)]
    unnamed x28 -> x1, local copies, waits for them, and re-layouts: 37.1 us -> 3.19 us
    dot_general x3 -> x0, matrix products: 29.1 us -> none  [the longest x1 14.6 us: local_block(): jnp.einsum('bsd,df->bsf', normed, w_in, preferred_element_type=jnp.float32)]
    unnamed x1 -> x0, other arithmetic: 26.7 us -> none
    convert_element_type x1 -> x0, local copies, waits for them, and re-layouts: 20.6 us -> none  [local_block(): (jnp.einsum('ij,bjc->bic', w_masked, value_seq, preferred_element_type=jn...]
    reduce_sum x4 -> x0, other arithmetic: 6.37 us -> none  [the longest x2 3.67 us: layer_norm(): var_val = jnp.mean(centered * centered, axis=-1, keepdims=True)]
where the time goes in v2:
time: 131 us
  Pallas kernels  128 us (98%)
  local copies, waits for them, and re-layouts  3.19 us (2%)
    pallas_call x1, Pallas kernels, local_block(): pl.pallas_call(functools.partial(kernel, n, side), out_shape=jax.ShapeDty...  128 us
    unnamed x1, local copies, waits for them, and re-layouts  3.19 us

profile of v2, /device:TPU:97, one launch (start us, length us, event | category | flops | bytes accessed | tf_op | source)
XLA Modules:
  0.0 131.2 jit_solution(3499945601525514064)
XLA Ops:
  0.0 128.0 %gmlp_block.1 = bf16[1024,1024]{1,0:T(8,128)(2,1)} custom-call(bf16[1024,1024]{1,0:T(8,128)(2,1)} %bitcast.10, f32[1,1024]{1,0:T(1,128)} %bitcast.14, f32[1,1024]{1,0:T(1,128)} %bitcast.15, bf16[1024,4096]{1,0:T(8,128)(2,1)} %wi_hbm.1, f32[1,4096]{1,0:T(1,128)} %bitcast.11, f32[1,2048]{1,0:T(1,128)} %bitcast.12, f32[1,2048]{1,0:T(1,128)} %bitcast.13, ...), custom_call_target="tpu_custom_call" | custom-call | tf_op jit(solution)/shard_map/gmlp_block/pallas_call | solution.py:333
  128.0 3.2 %copy.14 = bf16[32,32,1024]{2,1,0:T(8,128)(2,1)} copy(bf16[32,32,1024]{2,1,0:T(8,128)(2,1)} %bitcast.9) | data formatting | bytes 4194304

commit v3 on v1

v3 whole, which is shorter than its diff:
```python
import functools
import math

import jax
import jax.numpy as jnp
from jax import lax
from jax.experimental import pallas as pl
from jax.experimental.pallas import tpu as pltpu
from jax.sharding import PartitionSpec as P

LN_EPS = 1e-6
MESH = pl.DeviceIdType.MESH
F32 = jnp.float32
BF16 = jnp.bfloat16
CORES = 2
NB = 512
GELU_A = math.sqrt(2.0 / math.pi)


def gelu(a):
    return (0.5 * a) * (1.0 + jnp.tanh(a * (GELU_A + (GELU_A * 0.044715) * (a * a))))


def dot(a, b):
    return jnp.dot(a, b, preferred_element_type=F32)


def slot_offsets(side):
    def rank(o):
        da, db = (min(v, side - v) for v in o)
        two_legs = da > 0 and db > 0
        return (not two_legs, da * db if two_legs else 0, da != 0 or db != 0, da > db, -(da + db), o[0] + o[1] != side, o)
    return sorted(((da, db) for da in range(side) for db in range(side)), key=rank)


def kernel(n, side, x_hbm, ln1g, ln1b, wi_hbm, b_in, ln2g, ln2b, ws_hbm, bsp, mk_hbm, wo_hbm, b_out, out_hbm,
           xa, u, wv, wg, wo, wm, mk, vbuf, vn, g, st, bcol, bslot, q, ob,
           xsem, vsem, wsem, msem, gsem, osem, outsem, st_send, st_recv, dir_send, fw_send, fin):
    me = lax.axis_index("seq")
    c = me % CORES
    x = (me // CORES) % side
    y = me // (CORES * side)
    pos = xa.shape[0] // n
    chip = CORES * pos
    dim = xa.shape[1]
    gate = wo.shape[0]
    slots = slot_offsets(side)
    ns = len(slots)
    nrel = (side - 1) * (side - 1)
    home = slots.index((0, 0))
    fa = x + c * (y - x)
    fb = y + c * (x - y)

    def chip_of(da, db):
        a, b = (fa + da) % side, (fb + db) % side
        yy = b + c * (a - b)
        xx = a + c * (b - a)
        return yy * side + xx

    def dev(da, db, cc):
        return chip_of(da, db) * CORES + cc

    def back(s, same):
        da, db = ((side - v) % side for v in slots[s])
        return slots.index((da, db) if same else (db, da))

    def chip_rows(s):
        return pl.ds(pl.multiple_of(chip_of(*slots[s]) * chip, chip), chip)

    def srows(s, k=1):
        return pl.ds(s * chip, k * chip)

    def sub(s, cc):
        return pl.ds(pl.multiple_of(s * chip + cc * pos, pos), pos)

    def msg(d):
        return pl.ds(pl.multiple_of(d * pos, pos), pos)

    barrier = pltpu.get_barrier_semaphore()
    peers = [dev(d, 0, cc) for d in range(1, side) for cc in range(CORES)]
    peers += [dev(0, d, cc) for d in range(1, side) for cc in range(CORES)]
    peers += [dev(0, 0, 1 - c)]
    for p in peers:
        pl.semaphore_signal(barrier, inc=1, device_id={"seq": p}, device_id_type=MESH)

    def wcopy(s):
        return pltpu.make_async_copy(ws_hbm.at[chip_rows(s)], wm.at[srows(s)], wsem.at[s])

    def mcopy(s):
        return pltpu.make_async_copy(mk_hbm.at[chip_rows(s)], mk.at[srows(s)], msem.at[s])
    own_x = pltpu.make_async_copy(x_hbm.at[msg(me)], xa.at[sub(home, c)], xsem)
    wv_copy = pltpu.make_async_copy(wi_hbm.at[:, pl.ds(gate, gate)], wv, vsem)
    wg_copy = pltpu.make_async_copy(wi_hbm.at[:, pl.ds(0, gate)], wg, gsem)
    wo_copy = pltpu.make_async_copy(wo_hbm, wo, osem)
    own_x.start()
    wv_copy.start()

    def remote(src, dst, ssem, rsem, target):
        return pltpu.make_async_remote_copy(src_ref=src, dst_ref=dst, send_sem=ssem, recv_sem=rsem,
                                            device_id={"seq": target}, device_id_type=MESH)

    def landing(a, origin, r):
        return xa.at[sub(r, origin % CORES)] if a == 0 else out_hbm.at[msg(origin)]

    def stage(a, s):
        da, _ = slots[s]
        src = x_hbm.at[chip_rows(s)] if a == 0 else ob.at[srows(s)]
        return remote(src, st.at[a, s], st_send.at[a, s], st_recv.at[a, s], dev(da, 0, c))

    def to_core(same):
        return c if same else 1 - c

    def direct(a, s, same):
        r = back(s, same)
        cc = to_core(same)
        target = dev(*slots[s], cc)
        src = x_hbm.at[msg(target)] if a == 0 else ob.at[sub(s, cc)]
        return remote(src, landing(a, me, r), dir_send.at[a, CORES * (s - nrel) + same], fin.at[a, CORES * r + c], target)

    def directs(s):
        return (False,) if s == home else (True, False)

    def send(a, ss):
        for s in ss:
            if s < nrel:
                stage(a, s).start()
            else:
                for same in directs(s):
                    direct(a, s, same).start()

    def forward(a, s, same):
        da, db = slots[s]
        cc = to_core(same)
        r = back(s, same)
        origin = dev(side - da, 0, c)
        return remote(st.at[a, s, pl.ds(pl.multiple_of(cc * pos, pos), pos)], landing(a, origin, r),
                      fw_send.at[a, CORES * s + same], fin.at[a, CORES * r + c], dev(0, db, cc))

    relay_at = [0]

    def pump(k):
        for _ in range(k):
            a, s = divmod(relay_at[0], nrel)
            relay_at[0] += 1
            with jax.named_scope(f"r{a}_{s}"):
                stage(a, s).wait_recv()
                for same in (True, False):
                    forward(a, s, same).start()

    def wait_slots(a, ss):
        for r in ss:
            for oc in ([1 - c] if r == home else range(CORES)):
                remote(x_hbm.at[msg(me)], landing(a, dev(*slots[r], oc), r), dir_send.at[a, 0],
                       fin.at[a, CORES * r + oc], dev(0, 0, 1 - c)).wait_recv()

    lnr = 64

    def ln1(ss):
        for s in ss:
            v = xa[srows(s), :].astype(F32)
            cen = v - jnp.sum(v, axis=-1, keepdims=True) * (1.0 / dim)
            var = jnp.sum(cen * cen, axis=-1, keepdims=True) * (1.0 / dim)
            u[srows(s), :] = (cen * lax.rsqrt(var + LN_EPS) * ln1g[...] + ln1b[...]).astype(BF16)

    def value_cols(s0, k):
        def body(b, carry):
            cols = pl.ds(pl.multiple_of(b * NB, NB), NB)
            bcols = pl.ds(pl.multiple_of(gate + b * NB, NB), NB)
            vbuf[0:k * chip, cols] = gelu(dot(u[srows(s0, k), :], wv[:, cols]) + b_in[:, bcols]).astype(BF16)
            return carry
        lax.fori_loop(0, gate // NB, body, 0)

    lnr2 = 32

    def ln2(s0, k):
        for s in range(s0, s0 + k):
            base = chip_of(*slots[s]) * chip

            def body(i, carry):
                v = vbuf[pl.ds(pl.multiple_of((s - s0) * chip + i * lnr2, lnr2), lnr2), :].astype(F32)
                cen = v - jnp.sum(v, axis=-1, keepdims=True) * (1.0 / gate)
                var = jnp.sum(cen * cen, axis=-1, keepdims=True) * (1.0 / gate)
                r = pl.ds(pl.multiple_of(base + i * lnr2, lnr2), lnr2)
                vn[r, :] = (cen * lax.rsqrt(var + LN_EPS) * ln2g[...] + ln2b[...]).astype(BF16)
                return carry
            lax.fori_loop(0, chip // lnr2, body, 0, unroll=True)

    def gate_part(s0, k):
        def body(b, carry):
            cols = pl.ds(pl.multiple_of(b * NB, NB), NB)
            g[srows(s0, k), cols] = gelu(dot(u[srows(s0, k), :], wg[:, cols]) + b_in[:, cols]).astype(BF16)
            return carry
        lax.fori_loop(0, gate // NB, body, 0)

    def mask_weights():
        step = 64

        def body(k, carry):
            r = pl.ds(pl.multiple_of(k * step, step), step)
            wm[r, :] = jnp.where(mk[r, :] > 0, wm[r, :].astype(F32), 0.0).astype(BF16)
            return carry
        lax.fori_loop(0, wm.shape[0] // step, body, 0)
        for k in range(bsp.shape[1] // 128):
            blk = jnp.broadcast_to(bsp[:, k * 128:(k + 1) * 128], (128, 128))
            bcol[k * 128:(k + 1) * 128, :] = blk.T
        for s in range(ns):
            bslot[srows(s), :] = bcol[chip_rows(s), :]

    def spatial(s0, k):
        def body(b, carry):
            cols = pl.ds(pl.multiple_of(b * NB, NB), NB)
            sp = (dot(wm[srows(s0, k), :], vn[:, cols]) + bslot[srows(s0, k), 0:1]).astype(BF16)
            q[0:k * chip, cols] = (g[srows(s0, k), cols].astype(F32) * sp.astype(F32)).astype(BF16)
            return carry
        lax.fori_loop(0, gate // NB, body, 0)

    def project(s0, k):
        rows = srows(s0, k)

        def body(b, carry):
            cols = pl.ds(pl.multiple_of(b * NB, NB), NB)
            ob[rows, cols] = (xa[rows, cols].astype(F32) + (dot(q[0:k * chip, :], wo[:, cols]) + b_out[:, cols])).astype(BF16)
            return carry
        lax.fori_loop(0, dim // NB, body, 0)

    scope = jax.named_scope

    with scope("barrier"):
        pl.semaphore_wait(barrier, len(peers))
    send(0, range(ns))
    wg_copy.start()
    for s in range(ns):
        wcopy(s).start()
        mcopy(s).start()
    wo_copy.start()

    def front(s0, k, pumps=(0, 0, 0), wait_own=False):
        with scope(f"wait0_{s0}"):
            wait_slots(0, range(s0, s0 + k))
        with scope(f"ln1_{s0}"):
            ln1(range(s0, s0 + k))
        pump(pumps[0])
        with scope(f"value_{s0}"):
            value_cols(s0, k)
        pump(pumps[1])
        with scope(f"ln2_{s0}"):
            ln2(s0, k)
        pump(pumps[2])

    with scope("mask"):
        for s in range(ns):
            wcopy(s).wait()
            mcopy(s).wait()
        mask_weights()
    pump(2)
    with scope("w"):
        own_x.wait()
        wv_copy.wait()
        wg_copy.wait()
        wo_copy.wait()
    front(9, 4, (1, 1, 1))
    with scope("gate_9"):
        gate_part(9, 4)
    pump(2)
    front(0, 4, (1, 1, 0))
    with scope("gate_0"):
        gate_part(0, 4)
    front(4, 4)
    front(13, 3)
    front(8, 1)
    done = []
    for i, (s0, k) in enumerate(((0, 2), (2, 2), (4, 4), (8, 4), (12, 4))):
        if s0 == 4:
            with scope("gate_4"):
                gate_part(4, 4)
        if s0 == 8:
            with scope("gate_8"):
                gate_part(8, 1)
        if s0 == 12:
            with scope("gate_13"):
                gate_part(13, 3)
        with scope(f"spatial_{s0}"):
            spatial(s0, k)
        with scope(f"project_{s0}"):
            project(s0, k)
        send(1, range(s0, s0 + k))
        if s0 == 8:
            own_out = pltpu.make_async_copy(ob.at[sub(home, c)], out_hbm.at[msg(me)], outsem)
            own_out.start()
        pump((0, 0, 2, 3, 4)[i])
    assert relay_at[0] == 2 * nrel
    with scope("wait1"):
        wait_slots(1, range(ns))

    with scope("drain"):
        for a in range(2):
            for s in range(ns):
                if s < nrel:
                    stage(a, s).wait_send()
                    for same in (True, False):
                        forward(a, s, same).wait_send()
                else:
                    for same in directs(s):
                        direct(a, s, same).wait_send()
        own_out.wait()


def solution(mesh):
    n = mesh.shape['seq']
    side = math.isqrt(n // CORES)
    row_spec = P('data', 'seq', None)
    replicated = P()

    def local_block(act_in, ln1_scale, ln1_bias, w_in, b_in, ln2_scale, ln2_bias, w_spatial, b_spatial, causal_mask, w_out, b_out):
        batch, pos, dim = act_in.shape
        gate = w_out.shape[0]
        rows = batch * pos
        seq_len = w_spatial.shape[0]
        big = 4 * CORES * pos
        ns = side * side
        nrel = (side - 1) * (side - 1)
        if batch != n or side * side * CORES != n:
            raise ValueError('unexpected group')
        vm = pl.BlockSpec(memory_space=pltpu.VMEM)
        anyspec = pl.BlockSpec(memory_space=pl.ANY)
        dma = pltpu.SemaphoreType.DMA
        out = pl.pallas_call(
            functools.partial(kernel, n, side),
            out_shape=jax.ShapeDtypeStruct((rows, dim), BF16),
            in_specs=[anyspec, vm, vm, anyspec, vm, vm, vm, anyspec, vm, anyspec, anyspec, vm],
            out_specs=anyspec,
            scratch_shapes=[
                pltpu.VMEM((seq_len, dim), BF16), pltpu.VMEM((seq_len, dim), BF16),
                pltpu.VMEM((dim, gate), BF16), pltpu.VMEM((dim, gate), BF16), pltpu.VMEM((gate, dim), BF16),
                pltpu.VMEM((seq_len, seq_len), BF16), pltpu.VMEM((seq_len, seq_len), jnp.int32),
                pltpu.VMEM((big, gate), BF16),
                pltpu.VMEM((seq_len, gate), BF16), pltpu.VMEM((seq_len, gate), BF16),
                pltpu.VMEM((2, nrel, CORES * pos, dim), BF16),
                pltpu.VMEM((seq_len, 128), F32), pltpu.VMEM((seq_len, 128), F32),
                pltpu.VMEM((big, gate), BF16), pltpu.VMEM((seq_len, dim), BF16),
                dma, dma, dma((ns,)), dma((ns,)), dma, dma, dma,
                dma((2, nrel)), dma((2, nrel)), dma((2, CORES * (ns - nrel))),
                dma((2, CORES * nrel)), dma((2, n)),
            ],
            compiler_params=pltpu.CompilerParams(collective_id=0, has_side_effects=True, vmem_limit_bytes=66900000),
            name='gmlp_block',
        )(act_in.reshape(rows, dim), ln1_scale.reshape(1, -1), ln1_bias.reshape(1, -1), w_in, b_in.reshape(1, -1),
          ln2_scale.reshape(1, -1), ln2_bias.reshape(1, -1), w_spatial, b_spatial.reshape(1, -1), causal_mask, w_out,
          b_out.reshape(1, -1))
        return out.reshape(batch, pos, dim)

    return jax.shard_map(local_block, mesh=mesh, in_specs=(row_spec,) + (replicated,) * 11, out_specs=row_spec, check_vma=False)
```

time: 246 us -> 87.8 us (0.36); the launches traced: 242 us -> 87.6 us
  blocking collectives: 120 us -> 0 us
  Pallas kernels: 0 us -> 84.4 us
  local copies, waits for them, and re-layouts: 57.7 us -> 3.19 us
  other arithmetic: 34.8 us -> 0 us
  matrix products: 29.1 us -> 0 us
    all_to_all x2 -> x0, blocking collectives: 120 us -> none  [the longest x1 61.9 us: local_block(): value_seq = lax.all_to_all(value_norm, 'seq', 0, 1, tiled=True)]
    pallas_call x0 -> x1, Pallas kernels: none -> 84.4 us  [local_block(): pl.pallas_call(functools.partial(kernel, n, side), out_shape=jax.ShapeDty...]
    unnamed x28 -> x1, local copies, waits for them, and re-layouts: 37.1 us -> 3.19 us
    dot_general x3 -> x0, matrix products: 29.1 us -> none  [the longest x1 14.6 us: local_block(): jnp.einsum('bsd,df->bsf', normed, w_in, preferred_element_type=jnp.float32)]
    unnamed x1 -> x0, other arithmetic: 26.7 us -> none
    convert_element_type x1 -> x0, local copies, waits for them, and re-layouts: 20.6 us -> none  [local_block(): (jnp.einsum('ij,bjc->bic', w_masked, value_seq, preferred_element_type=jn...]
    reduce_sum x4 -> x0, other arithmetic: 6.37 us -> none  [the longest x2 3.67 us: layer_norm(): var_val = jnp.mean(centered * centered, axis=-1, keepdims=True)]
where the time goes in v3:
time: 87.8 us; the launch traced here: 87.6 us
  Pallas kernels  84.4 us (96%)
  local copies, waits for them, and re-layouts  3.19 us (4%)
    pallas_call x1, Pallas kernels, local_block(): pl.pallas_call(functools.partial(kernel, n, side), out_shape=jax.ShapeDty...  84.4 us
    unnamed x1, local copies, waits for them, and re-layouts  3.19 us

profile of v3, /device:TPU:97, one launch (start us, length us, event | category | flops | bytes accessed | tf_op | source)
XLA Modules:
  0.0 87.6 jit_solution(4096969987866481229)
XLA Ops:
  0.0 84.4 %gmlp_block.1 = bf16[1024,1024]{1,0:T(8,128)(2,1)} custom-call(bf16[1024,1024]{1,0:T(8,128)(2,1)} %bitcast.10, f32[1,1024]{1,0:T(1,128)} %bitcast.14, f32[1,1024]{1,0:T(1,128)} %bitcast.15, bf16[1024,4096]{1,0:T(8,128)(2,1)} %wi_hbm.1, f32[1,4096]{1,0:T(1,128)} %bitcast.11, f32[1,2048]{1,0:T(1,128)} %bitcast.12, f32[1,2048]{1,0:T(1,128)} %bitcast.13, ...), custom_call_target="tpu_custom_call" | custom-call | tf_op jit(solution)/shard_map/gmlp_block/pallas_call | solution.py:327
  84.4 3.2 %copy.14 = bf16[32,32,1024]{2,1,0:T(8,128)(2,1)} copy(bf16[32,32,1024]{2,1,0:T(8,128)(2,1)} %bitcast.9) | data formatting | bytes 4194304

commit v4 on v1

v4 whole, which is shorter than its diff:
```python
import functools
import math

import jax
import jax.numpy as jnp
from jax import lax
from jax.experimental import pallas as pl
from jax.experimental.pallas import tpu as pltpu
from jax.sharding import PartitionSpec as P

LN_EPS = 1e-6
MESH = pl.DeviceIdType.MESH
F32 = jnp.float32
BF16 = jnp.bfloat16
CORES = 2
NB = 256
GELU_A = math.sqrt(2.0 / math.pi)


def gelu(a):
    return (0.5 * a) * (1.0 + jnp.tanh(a * (GELU_A + (GELU_A * 0.044715) * (a * a))))


def dot(a, b):
    return jnp.dot(a, b, preferred_element_type=F32)


def slot_offsets(side):
    def rank(o):
        da, db = (min(v, side - v) for v in o)
        both = da > 0 and db > 0
        return (not both, da * db if both else 0, da != 0 or db != 0, da > db, da + db, o[0] + o[1] != side, o)
    return sorted(((da, db) for da in range(side) for db in range(side)), key=rank)


def kernel(n, side, x_hbm, ln1g_hbm, ln1b_hbm, wi_hbm, b_in_hbm, ln2g_hbm, ln2b_hbm, ws_hbm, bsp_hbm, mk_hbm, wo_hbm, b_out_hbm,
           out_hbm, ln1g, ln1b, b_in, ln2g, ln2b, bsp, b_out, psem,
           xa, u, wv, wg, wo, wm, mk, vbuf, vn, g, bcol, bslot, q, ob,
           acc0, acc1, xsem, vsem, wsem, msem, gsem, osem, outsem, sent, fin, vx_send, vx_recv):
    me = lax.axis_index("seq")
    c = me % CORES
    x = (me // CORES) % side
    y = me // (CORES * side)
    pos = xa.shape[0] // n
    dim = xa.shape[1]
    gate = wo.shape[0]
    slots = slot_offsets(side)
    ns = len(slots)
    home = slots.index((0, 0))
    seq = ns * pos
    fa = x + c * (y - x)
    fb = y + c * (x - y)

    def chip_of(da, db):
        a, b = (fa + da) % side, (fb + db) % side
        yy = b + c * (a - b)
        xx = a + c * (b - a)
        return yy * side + xx

    def dev(da, db):
        return chip_of(da, db) * CORES + c

    mate = me + 1 - 2 * c

    def back(k):
        return slots.index(tuple((side - v) % side for v in slots[k]))

    def row(s, k):
        return s * seq + k * pos

    def rows(s, k):
        return pl.ds(row(s, k), pos)

    def at(start, size):
        return pl.ds(pl.multiple_of(start, pos), size)

    def seq_rows(chip, s):
        return at((chip * CORES + s) * pos, pos)

    def position(k):
        return at(dev(*slots[k]) * pos, pos)

    barrier = pltpu.get_barrier_semaphore()
    peers = [dev(*o) for o in slots if o != (0, 0)] + [mate]
    for p in peers:
        pl.semaphore_signal(barrier, inc=1, device_id={"seq": p}, device_id_type=MESH)

    wcopies = [pltpu.make_async_copy(ws_hbm.at[position(k)], wm.at[rows(0, k)], wsem.at[k]) for k in range(ns)]
    wcopies += [pltpu.make_async_copy(mk_hbm.at[position(k)], mk.at[rows(0, k)], msem.at[k]) for k in range(ns)]
    own_x = [pltpu.make_async_copy(x_hbm.at[seq_rows(chip_of(0, 0), s)], xa.at[rows(s, home)], xsem.at[s]) for s in range(CORES)]
    own_out = [pltpu.make_async_copy(ob.at[rows(s, home)], out_hbm.at[seq_rows(chip_of(0, 0), s)], outsem.at[s]) for s in range(CORES)]
    wv_copy = pltpu.make_async_copy(wi_hbm.at[:, pl.ds(gate, gate)], wv, vsem)
    wg_copy = pltpu.make_async_copy(wi_hbm.at[:, pl.ds(0, gate)], wg, gsem)
    wo_copy = pltpu.make_async_copy(wo_hbm, wo, osem)
    small = [pltpu.make_async_copy(a, b, psem.at[i]) for i, (a, b) in enumerate((
        (ln1g_hbm, ln1g), (ln1b_hbm, ln1b), (b_in_hbm, b_in), (ln2g_hbm, ln2g), (ln2b_hbm, ln2b), (bsp_hbm, bsp), (b_out_hbm, b_out)))]

    def remote(src, dst, ssem, rsem, target):
        return pltpu.make_async_remote_copy(src_ref=src, dst_ref=dst, send_sem=ssem, recv_sem=rsem,
                                            device_id={"seq": target}, device_id_type=MESH)

    def source(a, s, k):
        return x_hbm.at[seq_rows(chip_of(*slots[k]), s)] if a == 0 else ob.at[rows(s, k)]

    def landing(a, s, k, origin_chip):
        return xa.at[rows(s, k)] if a == 0 else out_hbm.at[seq_rows(origin_chip, s)]

    def message(a, s, k):
        r = back(k)
        return remote(source(a, s, k), landing(a, s, r, chip_of(0, 0)), sent.at[a, s, k], fin.at[a, s, r], dev(*slots[k]))

    def send(a, s, ks):
        for k in ks:
            if k != home:
                message(a, s, k).start()

    def wait_from(a, s, ks):
        for k in ks:
            if k != home:
                remote(source(0, s, home), landing(a, s, k, chip_of(*slots[k])), sent.at[a, s, k], fin.at[a, s, k],
                       mate).wait_recv()

    def swap(s, k):
        return remote(vn.at[s, position(k)], vn.at[s, position(k)], vx_send.at[s, k], vx_recv.at[s, k], mate)

    def wait_swap(s, ks):
        for k in ks:
            da, db = slots[k]
            there = at((chip_of(db, da) * CORES + 1 - c) * pos, pos)
            remote(vn.at[s, position(home)], vn.at[s, there], vx_send.at[s, k], vx_recv.at[s, k], mate).wait_recv()

    accs = (acc0, acc1)
    lnr = 64
    lnr2 = 32

    def ln1(r0, k):
        for r in range(r0, r0 + k, lnr):
            v = xa[r:r + lnr, :].astype(F32)
            cen = v - jnp.sum(v, axis=-1, keepdims=True) * (1.0 / dim)
            var = jnp.sum(cen * cen, axis=-1, keepdims=True) * (1.0 / dim)
            u[r:r + lnr, :] = (cen * lax.rsqrt(var + LN_EPS) * ln1g[...] + ln1b[...]).astype(BF16)

    def steps(hi, product, finish):
        cols = [slice(b, b + NB) for b in range(0, hi, NB)]
        for i in range(len(cols) + 1):
            if i < len(cols):
                raw = product(cols[i])
                k = raw.shape[0]
                accs[i % 2][0:k, :] = raw
            if i > 0:
                finish(cols[i - 1], accs[(i - 1) % 2][0:k, :])

    def value_cols(r0, k):
        def finish(cols, raw):
            bcols = slice(gate + cols.start, gate + cols.stop)
            vbuf[0:k, cols] = gelu(raw + b_in[:, bcols]).astype(BF16)
        steps(gate, lambda cols: dot(u[r0:r0 + k, :], wv[:, cols]), finish)

    def ln2(s, ks):
        for i, k in enumerate(ks):
            v = vbuf[i * pos:(i + 1) * pos, :].astype(F32)
            cen = v - jnp.sum(v, axis=-1, keepdims=True) * (1.0 / gate)
            var = jnp.sum(cen * cen, axis=-1, keepdims=True) * (1.0 / gate)
            vn[s, position(k), :] = (cen * lax.rsqrt(var + LN_EPS) * ln2g[...] + ln2b[...]).astype(BF16)

    def gate_cols(r0, k):
        def finish(cols, raw):
            g[r0:r0 + k, cols] = gelu(raw + b_in[:, cols]).astype(BF16)
        steps(gate, lambda cols: dot(u[r0:r0 + k, :], wg[:, cols]), finish)

    def mask_weights():
        step = 64

        def mask_step(k, carry):
            r = pl.ds(pl.multiple_of(k * step, step), step)
            wm[r, :] = jnp.where(mk[r, :] > 0, wm[r, :].astype(F32), 0.0).astype(BF16)
            return carry
        lax.fori_loop(0, wm.shape[0] // step, mask_step, 0)
        for k in range(bsp.shape[1] // 128):
            blk = jnp.broadcast_to(bsp[:, k * 128:(k + 1) * 128], (128, 128))
            bcol[k * 128:(k + 1) * 128, :] = blk.T
        for k in range(ns):
            bslot[rows(0, k), :] = bcol[position(k), :]

    def spatial(s, w0, k):
        r0 = s * seq + w0

        def finish(cols, raw):
            sp = (raw + bslot[w0:w0 + k, 0:1]).astype(BF16)
            q[0:k, cols] = (g[r0:r0 + k, cols].astype(F32) * sp.astype(F32)).astype(BF16)
        steps(gate, lambda cols: dot(wm[w0:w0 + k, :], vn[s, :, cols]), finish)

    def project(s, w0, k):
        r0 = s * seq + w0

        def finish(cols, raw):
            ob[r0:r0 + k, cols] = (xa[r0:r0 + k, cols].astype(F32) + (raw + b_out[:, cols])).astype(BF16)
        steps(dim, lambda cols: dot(q[0:k, :], wo[:, cols]), finish)

    scope = jax.named_scope

    def front(s, i, k):
        with scope(f"wait0_{s}{i}"):
            if i <= home < i + k:
                own_x[s].wait()
            wait_from(0, s, range(i, i + k))
        with scope(f"ln1_{s}{i}"):
            ln1(s * seq + i * pos, k * pos)
        with scope(f"value_{s}{i}"):
            value_cols(s * seq + i * pos, k * pos)
        with scope(f"ln2_{s}{i}"):
            ln2(s, range(i, i + k))
        for j in range(i, i + k):
            swap(s, j).start()

    def gates(s, i, k):
        with scope(f"gate_{s}{i}"):
            gate_cols(s * seq + i * pos, k * pos)

    def back_part(s, i, k):
        with scope(f"spatial_{s}{i}"):
            spatial(s, i * pos, k * pos)
        with scope(f"project_{s}{i}"):
            project(s, i * pos, k * pos)
        send(1, s, range(i, i + k))
        if i <= home < i + k:
            own_out[s].start()

    for cp in small:
        cp.start()
    for cp in own_x:
        cp.start()
    for cp in wcopies:
        cp.start()
    with scope("barrier"):
        pl.semaphore_wait(barrier, len(peers))
    for s in range(CORES):
        send(0, s, range(ns))
    wv_copy.start()
    wg_copy.start()
    wo_copy.start()
    with scope("mask"):
        for cp in small + wcopies:
            cp.wait()
        mask_weights()
    with scope("w"):
        wv_copy.wait()
        wg_copy.wait()
        wo_copy.wait()
    front(0, 0, 8)
    gates(0, 0, 8)
    front(0, 8, 4)
    front(0, 12, 4)
    gates(0, 8, 8)
    with scope("swap_0"):
        wait_swap(0, range(ns))
    back_part(0, 0, 8)
    back_part(0, 8, 8)
    front(1, 0, 8)
    front(1, 8, 8)
    gates(1, 0, 8)
    gates(1, 8, 8)
    with scope("swap_1"):
        wait_swap(1, range(ns))
    back_part(1, 0, 4)
    back_part(1, 4, 4)
    back_part(1, 8, 4)
    back_part(1, 12, 4)
    with scope("wait1"):
        wait_from(1, 0, range(ns))
        wait_from(1, 1, range(ns))

    with scope("drain"):
        for s in range(CORES):
            for k in range(ns):
                if k != home:
                    for a in range(2):
                        message(a, s, k).wait_send()
                swap(s, k).wait_send()
            own_out[s].wait()


def solution(mesh):
    n = mesh.shape['seq']
    side = math.isqrt(n // CORES)
    row_spec = P('data', 'seq', None)
    replicated = P()

    def local_block(act_in, ln1_scale, ln1_bias, w_in, b_in, ln2_scale, ln2_bias, w_spatial, b_spatial, causal_mask, w_out, b_out):
        batch, pos, dim = act_in.shape
        gate = w_out.shape[0]
        rows = batch * pos
        seq_len = w_spatial.shape[0]
        ns = side * side
        part = 8 * pos
        if batch != n or side * side * CORES != n:
            raise ValueError('unexpected group')
        anyspec = pl.BlockSpec(memory_space=pl.ANY)
        dma = pltpu.SemaphoreType.DMA
        out = pl.pallas_call(
            functools.partial(kernel, n, side),
            out_shape=jax.ShapeDtypeStruct((rows, dim), BF16),
            in_specs=[anyspec] * 12,
            out_specs=anyspec,
            scratch_shapes=[
                pltpu.VMEM((1, dim), F32), pltpu.VMEM((1, dim), F32), pltpu.VMEM((1, 2 * gate), F32), pltpu.VMEM((1, gate), F32),
                pltpu.VMEM((1, gate), F32), pltpu.VMEM((1, seq_len), F32), pltpu.VMEM((1, dim), F32), dma((7,)),
                pltpu.VMEM((rows, dim), BF16), pltpu.VMEM((rows, dim), BF16),
                pltpu.VMEM((dim, gate), BF16), pltpu.VMEM((dim, gate), BF16), pltpu.VMEM((gate, dim), BF16),
                pltpu.VMEM((ns * pos, seq_len), BF16), pltpu.VMEM((ns * pos, seq_len), jnp.int32),
                pltpu.VMEM((part, gate), BF16),
                pltpu.VMEM((CORES, seq_len, gate), BF16), pltpu.VMEM((rows, gate), BF16),
                pltpu.VMEM((seq_len, 128), F32), pltpu.VMEM((ns * pos, 128), F32),
                pltpu.VMEM((part, gate), BF16), pltpu.VMEM((rows, dim), BF16),
                pltpu.VMEM((part, NB), F32), pltpu.VMEM((part, NB), F32),
                dma((CORES,)), dma, dma((ns,)), dma((ns,)), dma, dma, dma((CORES,)),
                dma((2, CORES, ns)), dma((2, CORES, ns)), dma((CORES, ns)), dma((CORES, ns)),
            ],
            compiler_params=pltpu.CompilerParams(collective_id=0, has_side_effects=True, vmem_limit_bytes=66900000),
            name='gmlp_block',
        )(act_in.reshape(rows, dim), ln1_scale.reshape(1, -1), ln1_bias.reshape(1, -1), w_in, b_in.reshape(1, -1),
          ln2_scale.reshape(1, -1), ln2_bias.reshape(1, -1), w_spatial, b_spatial.reshape(1, -1), causal_mask, w_out,
          b_out.reshape(1, -1))
        return out.reshape(batch, pos, dim)

    return jax.shard_map(local_block, mesh=mesh, in_specs=(row_spec,) + (replicated,) * 11, out_specs=row_spec, check_vma=False)
```

time: 246 us -> 66.3 us (0.27); the launches traced: 242 us -> 66 us
  blocking collectives: 120 us -> 0 us
  Pallas kernels: 0 us -> 62.9 us
  local copies, waits for them, and re-layouts: 57.7 us -> 3.19 us
  other arithmetic: 34.8 us -> 0 us
  matrix products: 29.1 us -> 0 us
    all_to_all x2 -> x0, blocking collectives: 120 us -> none  [the longest x1 61.9 us: local_block(): value_seq = lax.all_to_all(value_norm, 'seq', 0, 1, tiled=True)]
    pallas_call x0 -> x1, Pallas kernels: none -> 62.9 us  [local_block(): pl.pallas_call(functools.partial(kernel, n, side), out_shape=jax.ShapeDty...]
    unnamed x28 -> x1, local copies, waits for them, and re-layouts: 37.1 us -> 3.19 us
    dot_general x3 -> x0, matrix products: 29.1 us -> none  [the longest x1 14.6 us: local_block(): jnp.einsum('bsd,df->bsf', normed, w_in, preferred_element_type=jnp.float32)]
    unnamed x1 -> x0, other arithmetic: 26.7 us -> none
    convert_element_type x1 -> x0, local copies, waits for them, and re-layouts: 20.6 us -> none  [local_block(): (jnp.einsum('ij,bjc->bic', w_masked, value_seq, preferred_element_type=jn...]
    reduce_sum x4 -> x0, other arithmetic: 6.37 us -> none  [the longest x2 3.67 us: layer_norm(): var_val = jnp.mean(centered * centered, axis=-1, keepdims=True)]
where the time goes in v4:
time: 66.3 us; the launch traced here: 66 us
  Pallas kernels  62.9 us (95%)
  local copies, waits for them, and re-layouts  3.19 us (5%)
    pallas_call x1, Pallas kernels, local_block(): pl.pallas_call(functools.partial(kernel, n, side), out_shape=jax.ShapeDty...  62.9 us
    unnamed x1, local copies, waits for them, and re-layouts  3.19 us

profile of v4, /device:TPU:97, one launch (start us, length us, event | category | flops | bytes accessed | tf_op | source)
XLA Modules:
  0.0 66.0 jit_solution(3545553203794943964)
XLA Ops:
  0.0 62.9 %gmlp_block.1 = bf16[1024,1024]{1,0:T(8,128)(2,1)} custom-call(bf16[1024,1024]{1,0:T(8,128)(2,1)} %bitcast.10, f32[1,1024]{1,0:T(1,128)} %bitcast.14, f32[1,1024]{1,0:T(1,128)} %bitcast.15, bf16[1024,4096]{1,0:T(8,128)(2,1)} %wi_hbm.1, f32[1,4096]{1,0:T(1,128)} %bitcast.11, f32[1,2048]{1,0:T(1,128)} %bitcast.12, f32[1,2048]{1,0:T(1,128)} %bitcast.13, ...), custom_call_target="tpu_custom_call" | custom-call | tf_op jit(solution)/shard_map/gmlp_block/pallas_call | solution.py:300
  62.9 3.2 %copy.14 = bf16[32,32,1024]{2,1,0:T(8,128)(2,1)} copy(bf16[32,32,1024]{2,1,0:T(8,128)(2,1)} %bitcast.9) | data formatting | bytes 4194304

commit v5 on v4

--- a/solution.py
+++ b/solution.py
@@ -29,7 +29,7 @@
     def rank(o):
         da, db = (min(v, side - v) for v in o)
         both = da > 0 and db > 0
-        return (not both, da * db if both else 0, da != 0 or db != 0, da > db, da + db, o[0] + o[1] != side, o)
+        return (both, da != 0 or db != 0, da + db, da > db, o[0] + o[1] != side, o)
     return sorted(((da, db) for da in range(side) for db in range(side)), key=rank)
 
 
@@ -232,13 +232,13 @@
         cp.start()
     for cp in wcopies:
         cp.start()
+    wv_copy.start()
+    wg_copy.start()
+    wo_copy.start()
     with scope("barrier"):
         pl.semaphore_wait(barrier, len(peers))
     for s in range(CORES):
         send(0, s, range(ns))
-    wv_copy.start()
-    wg_copy.start()
-    wo_copy.start()
     with scope("mask"):
         for cp in small + wcopies:
             cp.wait()
@@ -254,18 +254,18 @@
     gates(0, 8, 8)
     with scope("swap_0"):
         wait_swap(0, range(ns))
+    back_part(0, 8, 4)
+    back_part(0, 12, 4)
     back_part(0, 0, 8)
-    back_part(0, 8, 8)
     front(1, 0, 8)
     front(1, 8, 8)
-    gates(1, 0, 8)
-    gates(1, 8, 8)
+    gates(1, 0, 16)
     with scope("swap_1"):
         wait_swap(1, range(ns))
+    back_part(1, 8, 4)
+    back_part(1, 12, 4)
     back_part(1, 0, 4)
     back_part(1, 4, 4)
-    back_part(1, 8, 4)
-    back_part(1, 12, 4)
     with scope("wait1"):
         wait_from(1, 0, range(ns))
         wait_from(1, 1, range(ns))
@@ -292,7 +292,7 @@
         rows = batch * pos
         seq_len = w_spatial.shape[0]
         ns = side * side
-        part = 8 * pos
+        part = 16 * pos
         if batch != n or side * side * CORES != n:
             raise ValueError('unexpected group')
         anyspec = pl.BlockSpec(memory_space=pl.ANY)

time: 66.3 us -> 64.4 us (0.971)
  Pallas kernels: 62.9 us -> 60.6 us
    pallas_call x1, Pallas kernels: 62.9 us -> 60.6 us  [local_block(): pl.pallas_call(functools.partial(kernel, n, side), out_shape=jax.ShapeDty...]
where the time goes in v5:
time: 64.4 us; the launch traced here: 63.8 us
  Pallas kernels  60.6 us (94%)
  local copies, waits for them, and re-layouts  3.19 us (5%)
    pallas_call x1, Pallas kernels, local_block(): pl.pallas_call(functools.partial(kernel, n, side), out_shape=jax.ShapeDty...  60.6 us
    unnamed x1, local copies, waits for them, and re-layouts  3.19 us

profile of v5, /device:TPU:97, one launch (start us, length us, event | category | flops | bytes accessed | tf_op | source)
XLA Modules:
  0.0 63.8 jit_solution(14948532661110355095)
XLA Ops:
  0.0 60.6 %gmlp_block.1 = bf16[1024,1024]{1,0:T(8,128)(2,1)} custom-call(bf16[1024,1024]{1,0:T(8,128)(2,1)} %bitcast.10, f32[1,1024]{1,0:T(1,128)} %bitcast.14, f32[1,1024]{1,0:T(1,128)} %bitcast.15, bf16[1024,4096]{1,0:T(8,128)(2,1)} %wi_hbm.1, f32[1,4096]{1,0:T(1,128)} %bitcast.11, f32[1,2048]{1,0:T(1,128)} %bitcast.12, f32[1,2048]{1,0:T(1,128)} %bitcast.13, ...), custom_call_target="tpu_custom_call" | custom-call | tf_op jit(solution)/shard_map/gmlp_block/pallas_call | solution.py:300
  60.6 3.2 %copy.14 = bf16[32,32,1024]{2,1,0:T(8,128)(2,1)} copy(bf16[32,32,1024]{2,1,0:T(8,128)(2,1)} %bitcast.9) | data formatting | bytes 4194304

commit v6 on v5

--- a/solution.py
+++ b/solution.py
@@ -299,8 +299,8 @@
         dma = pltpu.SemaphoreType.DMA
         out = pl.pallas_call(
             functools.partial(kernel, n, side),
-            out_shape=jax.ShapeDtypeStruct((rows, dim), BF16),
-            in_specs=[anyspec] * 12,
+            out_shape=pltpu.VMEM((rows, dim), BF16),
+            in_specs=[pl.BlockSpec(memory_space=pltpu.HBM)] * 12,
             out_specs=anyspec,
             scratch_shapes=[
                 pltpu.VMEM((1, dim), F32), pltpu.VMEM((1, dim), F32), pltpu.VMEM((1, 2 * gate), F32), pltpu.VMEM((1, gate), F32),
@@ -316,7 +316,7 @@
                 dma((CORES,)), dma, dma((ns,)), dma((ns,)), dma, dma, dma((CORES,)),
                 dma((2, CORES, ns)), dma((2, CORES, ns)), dma((CORES, ns)), dma((CORES, ns)),
             ],
-            compiler_params=pltpu.CompilerParams(collective_id=0, has_side_effects=True, vmem_limit_bytes=66900000),
+            compiler_params=pltpu.CompilerParams(collective_id=0, has_side_effects=True, vmem_limit_bytes=60000000),
             name='gmlp_block',
         )(act_in.reshape(rows, dim), ln1_scale.reshape(1, -1), ln1_bias.reshape(1, -1), w_in, b_in.reshape(1, -1),
           ln2_scale.reshape(1, -1), ln2_bias.reshape(1, -1), w_spatial, b_spatial.reshape(1, -1), causal_mask, w_out,

time: 64.4 us -> 62.6 us (0.972)
  local copies, waits for them, and re-layouts: 3.19 us -> 1.32 us
    unnamed x1, local copies, waits for them, and re-layouts: 3.19 us -> 1.32 us
where the time goes in v6:
time: 62.6 us; the launch traced here: 62.2 us
  Pallas kernels  60.9 us (97%)
  local copies, waits for them, and re-layouts  1.32 us (2%)
    pallas_call x1, Pallas kernels, local_block(): pl.pallas_call(functools.partial(kernel, n, side), out_shape=pltpu.VMEM((...  60.9 us
    unnamed x1, local copies, waits for them, and re-layouts  1.32 us

profile of v6, /device:TPU:97, one launch (start us, length us, event | category | flops | bytes accessed | tf_op | source)
XLA Modules:
  0.0 62.2 jit_solution(9241202487034505568)
XLA Ops:
  0.0 60.9 %gmlp_block.1 = bf16[1024,1024]{1,0:T(8,128)(2,1)S(1)} custom-call(bf16[1024,1024]{1,0:T(8,128)(2,1)} %bitcast.10, f32[1,1024]{1,0:T(1,128)} %bitcast.14, f32[1,1024]{1,0:T(1,128)} %bitcast.15, bf16[1024,4096]{1,0:T(8,128)(2,1)} %wi_hbm.1, f32[1,4096]{1,0:T(1,128)} %bitcast.11, f32[1,2048]{1,0:T(1,128)} %bitcast.12, f32[1,2048]{1,0:T(1,128)} %bitcast.13, ...), custom_call_target="tpu_custom_call" | custom-call | tf_op jit(solution)/shard_map/gmlp_block/pallas_call | solution.py:300
  60.9 1.3 %copy.14 = bf16[32,32,1024]{2,1,0:T(8,128)(2,1)} copy(bf16[32,32,1024]{2,1,0:T(8,128)(2,1)S(1)} %bitcast.9) | data formatting | bytes 4194304

commit v7 on v6

--- a/solution.py
+++ b/solution.py
@@ -237,8 +237,7 @@
     wo_copy.start()
     with scope("barrier"):
         pl.semaphore_wait(barrier, len(peers))
-    for s in range(CORES):
-        send(0, s, range(ns))
+    send(0, 0, range(ns))
     with scope("mask"):
         for cp in small + wcopies:
             cp.wait()
@@ -248,6 +247,7 @@
         wg_copy.wait()
         wo_copy.wait()
     front(0, 0, 8)
+    send(0, 1, range(ns))
     gates(0, 0, 8)
     front(0, 8, 4)
     front(0, 12, 4)

time: 62.6 us -> 63.4 us (1.013)
  Pallas kernels: 60.9 us -> 62 us
    pallas_call x1, Pallas kernels: 60.9 us -> 62 us  [local_block(): pl.pallas_call(functools.partial(kernel, n, side), out_shape=pltpu.VMEM((...]
where the time goes in v7:
time: 63.4 us
  Pallas kernels  62 us (98%)
  local copies, waits for them, and re-layouts  1.32 us (2%)
    pallas_call x1, Pallas kernels, local_block(): pl.pallas_call(functools.partial(kernel, n, side), out_shape=pltpu.VMEM((...  62 us
    unnamed x1, local copies, waits for them, and re-layouts  1.32 us

profile of v7, /device:TPU:97, one launch (start us, length us, event | category | flops | bytes accessed | tf_op | source)
XLA Modules:
  0.0 63.4 jit_solution(12154268649304827750)
XLA Ops:
  0.0 62.0 %gmlp_block.1 = bf16[1024,1024]{1,0:T(8,128)(2,1)S(1)} custom-call(bf16[1024,1024]{1,0:T(8,128)(2,1)} %bitcast.10, f32[1,1024]{1,0:T(1,128)} %bitcast.14, f32[1,1024]{1,0:T(1,128)} %bitcast.15, bf16[1024,4096]{1,0:T(8,128)(2,1)} %wi_hbm.1, f32[1,4096]{1,0:T(1,128)} %bitcast.11, f32[1,2048]{1,0:T(1,128)} %bitcast.12, f32[1,2048]{1,0:T(1,128)} %bitcast.13, ...), custom_call_target="tpu_custom_call" | custom-call | tf_op jit(solution)/shard_map/gmlp_block/pallas_call | solution.py:300
  62.1 1.3 %copy.14 = bf16[32,32,1024]{2,1,0:T(8,128)(2,1)} copy(bf16[32,32,1024]{2,1,0:T(8,128)(2,1)S(1)} %bitcast.9) | data formatting | bytes 4194304
